TPU v7x, 256 devices: a whole 4x4x8 slice. The times are simulated.
256 devices in a mesh: vpair: 16 (over x, y), rank: 16 (over z, core).
Axes of the slice: x: 4, y: 4, z: 8, core: 2. Of those that a mesh axis runs over, the one named last changes fastest.
Arguments:
- amplitudes: bfloat16 [8, 1200, 1200], P(None, 'vpair', 'rank'), may hold values from -6 to 6
- factors: bfloat16 [1200, 8192], P('vpair', 'rank'), may hold values from -0.1875 to 0.1875
- kernel: bfloat16 [8192, 8192], P('vpair', 'rank'), may hold values from -0.875 to 0.875
- other_terms: float32 [8, 1200, 1200], P(None, 'vpair'), may hold values from -6 to 6
- virt_energy: float32 [1200], replicated, may hold values from 0.2 to 4
- pair_energy: float32 [8], replicated, may hold values from -3 to -0.5
Outputs:
- residual: float32 [8, 1200, 1200], P(None, 'vpair')
- update_rms: float32 [], replicated
All inputs are finite; a program needn't handle non-finite values.
Results may differ from a plain program's by a relative error of at most 0.0035.
Values may be sent and summed in bfloat16 or wider, within the bound.
A program may use at most 192 MiB of HBM per device.

v0:
```python
import jax
import jax.numpy as jnp
from jax import lax
from jax.sharding import Mesh
from jax.sharding import PartitionSpec as P

VPAIR = ("vpair_0", "vpair_1")
epsilon = 1e-06


def sent_to_all(shard, axis):
    copies = jnp.broadcast_to(shard, (lax.axis_size(axis), *shard.shape))
    return lax.all_to_all(copies, axis, split_axis=0, concat_axis=0, tiled=True)


def in_order(tiles, dim):
    lengths = list(tiles.shape[1:])
    lengths[dim] *= tiles.shape[0]
    return jnp.moveaxis(tiles, 0, dim).reshape(lengths)


def collect(shard, axis, dim):
    tiles = sent_to_all(shard, axis)
    return in_order(tiles, dim)


def filled_up(lines, count):
    spare = -len(lines) % count
    return jnp.pad(lines, [(0, spare)] + [(0, 0)] * (lines.ndim - 1))


def total_of(shard, axis):
    lines = shard.reshape(-1, *shard.shape[1:][-1:])
    padded = filled_up(lines, lax.axis_size(axis))
    own = lax.psum_scatter(padded, axis, scatter_dimension=0, tiled=True)
    whole = lax.all_gather(own, axis, axis=0, tiled=True)
    return whole[: len(lines)].reshape(shard.shape)


def one_axis_at_a_time(shard, axes):
    for axis in axes:
        shard = lax.psum(shard, axis)
    return shard


def shards(amplitudes, factors, kernel, other_terms, virt_energy, pair_energy):
    vpair_count = lax.axis_size(VPAIR)
    pair_count = amplitudes.shape[0]
    row_block = amplitudes.shape[1]
    virt_count = row_block * vpair_count
    right_block = kernel.shape[1]
    factor_rows = collect(factors, "rank", 1)
    factor_full = lax.all_gather(factor_rows, VPAIR, axis=0, tiled=True)
    factor_cols = lax.dynamic_slice_in_dim(
        factor_full, lax.axis_index("rank") * right_block, right_block, 1
    )
    half_done = jnp.einsum(
        "ons,sh->onh",
        collect(amplitudes, "rank", 2),
        factor_cols,
        preferred_element_type=jnp.float32,
    ).astype(jnp.bfloat16)
    kernel_sub = lax.all_to_all(kernel, VPAIR, split_axis=1, concat_axis=0, tiled=True).astype(
        jnp.float32
    )
    coupled = jnp.einsum(
        "cp,icq->ipq",
        factor_full,
        lax.all_to_all(half_done, VPAIR, split_axis=2, concat_axis=1, tiled=True),
        preferred_element_type=jnp.float32,
    )
    weighted = (kernel_sub[None] * coupled).astype(jnp.bfloat16)
    ladder_half = jnp.einsum(
        "ap,ipq->iaq", factor_full, weighted, preferred_element_type=jnp.float32
    ).astype(jnp.bfloat16)
    back_half = lax.all_to_all(ladder_half, VPAIR, split_axis=1, concat_axis=2, tiled=True)
    partial_value = jnp.einsum(
        "iaq,bq->iab", back_half, factor_cols, preferred_element_type=jnp.float32
    )
    row_energy = lax.dynamic_slice_in_dim(
        virt_energy, lax.axis_index(VPAIR) * row_block, row_block, 0
    )
    ladder = total_of(partial_value, "rank")
    residual = other_terms + ladder
    denominator = (
        row_energy[None, :, None] + virt_energy[None, None, :] - pair_energy[:, None, None]
    )
    update = residual / denominator
    squares = one_axis_at_a_time(jnp.sum(update * update), VPAIR)
    update_rms = jnp.sqrt(squares / (pair_count * virt_count * virt_count) + epsilon)
    return (residual, update_rms)


def solution(mesh):
    torus = Mesh(mesh.devices.reshape(4, 4, mesh.shape["rank"]), ("vpair_0", "vpair_1", "rank"))
    return jax.shard_map(
        shards,
        mesh=torus,
        in_specs=(
            P(None, VPAIR, "rank"),
            P(VPAIR, "rank"),
            P(VPAIR, "rank"),
            P(None, VPAIR, None),
            P(),
            P(),
        ),
        out_specs=(P(None, VPAIR, None), P()),
        check_vma=False,
    )
```

profile of v0, /device:TPU:32, one launch (start us, length us, event | category | flops | bytes accessed | tf_op | source)
XLA Modules:
  0.0 428.2 jit_solution(5133619606905226404)
XLA Ops:
  7.2 0.0 all-gather.5.cloned.1.call-start
  7.2 1.0 broadcast_in_dim.4
  8.2 40.6 %all_to_all.56 = bf16[16,75,512]{2,1,0:T(8,128)(2,1)S(1)} all-to-all(bf16[16,75,512]{2,1,0:T(8,128)(2,1)S(1)} %broadcast_in_dim.4), channel_id=1, replica_groups=mesh['vpair_0'=4,'vpair_1'=4,'rank'=16] {'rank'}, dimensions={0} | all-to-all | bytes 2457600 | tf_op jit(solution)/shard_map/all_to_all | solution.py:13
  48.8 0.0 copy-start.1
  48.8 0.7 copy.30
  49.5 1.7 reshape.63
  51.2 0.0 all-gather.5.cloned.1.call-update
  51.2 0.0 copy-done.1
  51.2 0.0 copy-start
  51.2 1.8 broadcast_in_dim.5
  53.0 5.0 %all-to-all-start.2 = ((bf16[16,8,75,75]{3,1,2,0:T(8,128)(2,1)}), bf16[16,8,75,75]{3,1,2,0:T(8,128)(2,1)S(1)}, u32[]{:S(2)}, u32[]{:S(2)}) async-start(bf16[16,8,75,75]{3,1,2,0:T(8,128)(2,1)} %broadcast_in_dim.5), calls=%async_computation.2 | async-start | bytes 4915200 | tf_op jit(solution)/shard_map/all_to_all | solution.py:13
  58.0 0.0 copy-done
  58.0 1.0 copy.28
  59.0 53.9 %all-to-all-done.2 = bf16[16,8,75,75]{3,1,2,0:T(8,128)(2,1)S(1)} async-done(((bf16[16,8,75,75]{3,1,2,0:T(8,128)(2,1)}), bf16[16,8,75,75]{3,1,2,0:T(8,128)(2,1)S(1)}, u32[]{:S(2)}, u32[]{:S(2)}) %all-to-all-start.2) | async-done | bytes 1440032 | tf_op jit(solution)/shard_map/all_to_all | solution.py:13
  112.9 7.0 %all-to-all-start = ((bf16[512,16,32]{0,2,1:T(8,128)(2,1)}), bf16[512,16,32]{0,2,1:T(8,128)(2,1)S(1)}, u32[]{:S(2)}, u32[]{:S(2)}) async-start(bf16[512,16,32]{0,2,1:T(8,128)(2,1)} %bitcast), calls=%async_computation | async-start | bytes 1048576 | tf_op jit(solution)/shard_map/all_to_all | solution.py:63
  119.9 1.8 copy.40
  121.7 4.2 reshape.70
  125.9 67.6 %all-gather.5.cloned.1.call-done = bf16[16,75,8192]{2,1,0:T(8,128)(2,1)} async-done(((bf16[1,75,8192]{2,1,0:T(8,128)(2,1)}), bf16[16,75,8192]{2,1,0:T(8,128)(2,1)}) %all-gather.5.cloned.1.call-update) | async-done | bytes 19660816 | tf_op jit(solution)/shard_map/all_gather | solution.py:53
  193.5 22.4 %reshape.64 = bf16[1200,8192]{1,0:T(8,128)(2,1)} reshape(bf16[16,75,8192]{2,1,0:T(8,128)(2,1)} %all-gather.5.cloned.1.call-done) | data formatting | bytes 39321600
  215.9 2.3 fusion.4
  218.2 1.5 copy.33
  219.7 0.0 all-to-all-done
  219.7 5.3 %all-to-all-start.3 = ((bf16[8,75,512]{1,0,2:T(8,128)(2,1)}), bf16[8,75,512]{1,0,2:T(8,128)(2,1)S(1)}, u32[]{:S(2)}, u32[]{:S(2)}) async-start(bf16[8,75,512]{1,0,2:T(8,128)(2,1)} %copy.33), calls=%async_computation.3 | async-start | bytes 2097152 | tf_op jit(solution)/shard_map/all_to_all | solution.py:69
  225.0 0.2 all-gather.7.cloned.1.call-start
  225.2 0.1 convert_bitcast_fusion
  225.3 0.1 copy.43
  225.4 22.3 %reshape.69 = bf16[1200,8192,1]{1,0,2:T(8,128)(2,1)} reshape(bf16[16,75,8192]{2,1,0:T(8,128)(2,1)} %all-gather.5.cloned.1.call-done) | data formatting | bytes 39321600
  247.8 0.0 all-to-all-done.3
  247.8 0.7 copy.35
  248.5 1.3 all_to_all.47
  249.8 17.8 %fusion.3 = bf16[8,1200,32]{1,2,0:T(8,128)(2,1)} fusion(bf16[1200,8192,1]{1,0,2:T(8,128)(2,1)} %reshape.69, bf16[8,1200,32]{1,2,0:T(8,128)(2,1)S(1)} %all_to_all.47, f32[8192,32]{0,1:T(8,128)S(1)} %bitcast.57), kind=kOutput, calls=%fused_computation.6 | convolution fusion | flops 10070831104 | bytes 21938176 | tf_op jit(solution)/shard_map/ap,ipq->iaq/dot_general | solution.py:73
  267.6 3.9 copy.36
  271.5 2.4 reshape.73
  273.9 18.8 %all_to_all.57 = bf16[16,2,9600]{2,1,0:T(2,128)(2,1)} all-to-all(bf16[16,2,9600]{2,1,0:T(2,128)(2,1)S(1)} %reshape.73), channel_id=1, replica_groups=mesh['vpair_0'=4,'vpair_1'=4,'rank'=16] {'vpair_0','vpair_1'}, dimensions={0} | all-to-all | bytes 1228800 | tf_op jit(solution)/shard_map/all_to_all | solution.py:76
  292.7 3.6 reshape.74
  296.3 2.8 copy.37
  299.1 0.8 dot_general.17
  299.9 2.4 fusion.6
  302.3 0.2 pad.4
  302.5 0.0 copy-start.4
  302.5 0.0 copy-start.2
  302.6 30.6 %fusion = f32[40,1200]{1,0:T(8,128)S(1)} fusion(f32[608,1200]{1,0:T(8,128)S(1)} %pad.4), kind=kCustom, calls=%all-reduce-scatter | all-reduce-scatter fusion | flops 768001 | bytes 3111424
  333.2 1.9 collective-permute-start
  335.2 0.0 copy-done.4
  335.2 0.6 dynamic-slice.4
  336.4 3.5 collective-permute-done
  339.9 0.2 concatenate
  340.1 0.7 dynamic-slice_bitcast_fusion
  340.8 0.0 all-gather.7.cloned.1.call-update
  340.8 0.0 copy-done.2
  340.8 0.1 dynamic_slice.7
  340.9 0.9 broadcast_add_fusion
  341.8 39.6 %all-gather.7.cloned.1.call-done = f32[16,38,1200]{2,1,0:T(8,128)} async-done(((f32[1,38,1200]{2,1,0:T(8,128)}), f32[16,38,1200]{2,1,0:T(8,128)}) %all-gather.7.cloned.1.call-update) | async-done | bytes 2918416 | tf_op jit(solution)/shard_map/all_gather | solution.py:36
  381.4 2.1 reshape.66
  383.5 1.8 slice.4
  385.3 0.0 copy-start.3
  385.4 3.9 reshape.61
  389.3 0.0 copy-done.3
  389.3 4.8 %multiply_reduce_fusion = (f32[]{:T(128)}, f32[8,75,1200]{2,1,0:T(8,128)S(1)}) fusion(f32[8]{0:T(128)S(1)} %copy-done.3, f32[75,1200]{1,0:T(8,128)} %broadcast_add_fusion, f32[8,75,1200]{2,1,0:T(8,128)} %reshape.61, f32[8,75,1200]{2,0,1:T(8,128)} %param.9), kind=kLoop, calls=%fused_computation.4 | loop fusion | flops 3599999 | bytes 9000036 | tf_op jit(solution)/shard_map/reduce_sum | solution.py:89
  394.1 11.0 %psum.14 = f32[]{:T(128)} all-reduce(f32[]{:T(128)} %get-tuple-element.8), channel_id=1, replica_groups=mesh['vpair_0'=4,'vpair_1'=4,'rank'=16] {'vpair_0'}, use_global_device_ids=true, to_apply=%region_2.3 | all-reduce | flops 1 | bytes 8 | tf_op jit(solution)/shard_map/psum | solution.py:42
  405.1 3.4 copy.39
  408.5 11.1 %psum.15 = f32[]{:T(128)} all-reduce(f32[]{:T(128)} %psum.14), channel_id=1, replica_groups=mesh['vpair_0'=4,'vpair_1'=4,'rank'=16] {'vpair_1'}, use_global_device_ids=true, to_apply=%region_3.4 | all-reduce | flops 1 | bytes 8 | tf_op jit(solution)/shard_map/psum | solution.py:42
  (1 shorter events, 0.0 us)
Async XLA Ops:
  7.2 186.3 %all-gather.5.cloned.1.call-start = ((), (), s32[]{:S(2)}) async-start(), calls=%async_computation.5 | async-start | bytes 22282240 | tf_op jit(solution)/shard_map/all_gather | solution.py:53
  48.8 2.4 copy-start.1
  51.2 6.7 %copy-start = (bf16[512,512]{1,0:T(8,128)(2,1)S(1)}, bf16[512,512]{1,0:T(8,128)(2,1)}, u32[]{:S(2)}) copy-start(bf16[512,512]{1,0:T(8,128)(2,1)} %param.8) | copy-start | bytes 1572868
  53.0 59.9 %all-to-all-start.2 = ((bf16[16,8,75,75]{3,1,2,0:T(8,128)(2,1)}), bf16[16,8,75,75]{3,1,2,0:T(8,128)(2,1)S(1)}, u32[]{:S(2)}, u32[]{:S(2)}) async-start(bf16[16,8,75,75]{3,1,2,0:T(8,128)(2,1)} %broadcast_in_dim.5), calls=%async_computation.2 | async-start | bytes 4915200 | tf_op jit(solution)/shard_map/all_to_all | solution.py:13
  112.9 106.9 %all-to-all-start = ((bf16[512,16,32]{0,2,1:T(8,128)(2,1)}), bf16[512,16,32]{0,2,1:T(8,128)(2,1)S(1)}, u32[]{:S(2)}, u32[]{:S(2)}) async-start(bf16[512,16,32]{0,2,1:T(8,128)(2,1)} %bitcast), calls=%async_computation | async-start | bytes 1048576 | tf_op jit(solution)/shard_map/all_to_all | solution.py:63
  219.7 28.1 %all-to-all-start.3 = ((bf16[8,75,512]{1,0,2:T(8,128)(2,1)}), bf16[8,75,512]{1,0,2:T(8,128)(2,1)S(1)}, u32[]{:S(2)}, u32[]{:S(2)}) async-start(bf16[8,75,512]{1,0,2:T(8,128)(2,1)} %copy.33), calls=%async_computation.3 | async-start | bytes 2097152 | tf_op jit(solution)/shard_map/all_to_all | solution.py:69
  225.0 156.4 %all-gather.7.cloned.1.call-start = ((), (), s32[]{:S(2)}) async-start(), calls=%async_computation.6 | async-start | bytes 3481600 | tf_op jit(solution)/shard_map/all_gather | solution.py:36
  302.5 32.6 %copy-start.4 = (u32[256]{0:T(256)S(1)}, u32[256]{0:T(256)}, u32[]{:S(2)}) copy-start(u32[256]{0:T(256)} %constant.40) | copy-start | bytes 3076
  302.5 38.3 %copy-start.2 = (f32[1200]{0:T(1024)S(1)}, f32[1200]{0:T(1024)}, u32[]{:S(2)}) copy-start(f32[1200]{0:T(1024)} %param.10) | copy-start | bytes 14404
  333.2 6.6 %collective-permute-start = (f32[30,1200]{1,0:T(8,128)S(1)}, f32[30,1200]{1,0:T(8,128)S(1)}, u32[]{:S(2)}, u32[]{:S(2)}) collective-permute-start(f32[30,1200]{1,0:T(8,128)S(1)} %slice.5), channel_id=1, source_target_pairs={{0,1},{1,2},{2,3},{3,4},{4,5},{5,6},{6,7},{7,8},{8,9},{9,10},{10,1... | collective-permute-start | bytes 432008
  385.3 3.9 copy-start.3
Sparse Core Ops, SparseCore 0:
  51.3 142.0 all-gather.4
  340.9 40.4 all-gather.6
where the time goes:
time: 429 us; the launch traced here: 428 us
  waiting for transfers between devices  165 us (38%)
  blocking collectives  112 us (26%)
  local copies, waits for them, and re-layouts  87.1 us (20%)
  matrix products  22.5 us (5%)
  starting transfers between devices  19.4 us (5%)
  between operations  16.7 us (4%)
  other arithmetic  5.74 us (1%)
    all_gather x1, waiting for transfers between devices, shards(): factor_full = lax.all_gather(factor_rows, VPAIR, axis=0, tiled=True)  67.6 us
    unnamed x22, local copies, waits for them, and re-layouts  60.5 us
    all_to_all x1, waiting for transfers between devices, sent_to_all(): return lax.all_to_all(copies, axis, split_axis=0, concat_axis=0, tiled=True)  53.9 us
    all_to_all x1, blocking collectives, sent_to_all(): return lax.all_to_all(copies, axis, split_axis=0, concat_axis=0, tiled=True)  40.6 us
    all_gather x1, waiting for transfers between devices, total_of(): whole = lax.all_gather(own, axis, axis=0, tiled=True)  39.6 us
    unnamed x1, blocking collectives  30.6 us
    psum x2, blocking collectives, one_axis_at_a_time(): shard = lax.psum(shard, axis)  22.1 us
    all_to_all x1, blocking collectives, shards(): lax.all_to_all(ladder_half, VPAIR, split_axis=1, concat_axis=2, tiled=True)  18.8 us
  transfers between devices with their start and end apart: 6, of which 4 were waited for; matrix products, arithmetic and copies ran while one was open for 14% of the time, Pallas kernels for 0%

commit v1 on v0

--- a/solution.py
+++ b/solution.py
@@ -73,7 +73,12 @@
     ladder_half = jnp.einsum(
         "ap,ipq->iaq", factor_full, weighted, preferred_element_type=jnp.float32
     ).astype(jnp.bfloat16)
-    back_half = lax.all_to_all(ladder_half, VPAIR, split_axis=1, concat_axis=2, tiled=True)
+    back_half = jnp.concatenate(
+        lax.all_to_all(
+            jnp.stack(jnp.split(ladder_half, lax.axis_size(VPAIR), axis=1)), VPAIR, 0, 0
+        ),
+        axis=2,
+    )
     partial_value = jnp.einsum(
         "iaq,bq->iab", back_half, factor_cols, preferred_element_type=jnp.float32
     )

time: 429 us -> 423 us (0.986)
  local copies, waits for them, and re-layouts: 87.1 us -> 77.2 us
    all_to_all x1, blocking collectives: 18.8 us -> 23.4 us  [shards(): lax.all_to_all(jnp.stack(jnp.split(ladder_half, lax.axis_size(VPAIR), axi...]
    unnamed x22 -> x35, local copies, waits for them, and re-layouts: 60.5 us -> 55.9 us
where the time goes in v1:
time: 423 us; the launch traced here: 422 us
  waiting for transfers between devices  165 us (39%)
  blocking collectives  116 us (27%)
  local copies, waits for them, and re-layouts  77.2 us (18%)
  matrix products  21.8 us (5%)
  starting transfers between devices  19.4 us (5%)
  between operations  16.8 us (4%)
  other arithmetic  5.74 us (1%)
    all_gather x1, waiting for transfers between devices, shards(): factor_full = lax.all_gather(factor_rows, VPAIR, axis=0, tiled=True)  67.6 us
    unnamed x35, local copies, waits for them, and re-layouts  55.9 us
    all_to_all x1, waiting for transfers between devices, sent_to_all(): return lax.all_to_all(copies, axis, split_axis=0, concat_axis=0, tiled=True)  53.9 us
    all_to_all x1, blocking collectives, sent_to_all(): return lax.all_to_all(copies, axis, split_axis=0, concat_axis=0, tiled=True)  40.6 us
    all_gather x1, waiting for transfers between devices, total_of(): whole = lax.all_gather(own, axis, axis=0, tiled=True)  40 us
    unnamed x1, blocking collectives  30.2 us
    all_to_all x1, blocking collectives, shards(): lax.all_to_all(jnp.stack(jnp.split(ladder_half, lax.axis_size(VPAIR), axi...  23.4 us
    psum x2, blocking collectives, one_axis_at_a_time(): shard = lax.psum(shard, axis)  22.1 us
  transfers between devices with their start and end apart: 6, of which 4 were waited for; matrix products, arithmetic and copies ran while one was open for 14% of the time, Pallas kernels for 0%

profile of v1, /device:TPU:32, one launch (start us, length us, event | category | flops | bytes accessed | tf_op | source)
XLA Modules:
  0.0 422.3 jit_solution(18273304703761659697)
XLA Ops:
  7.2 0.0 all-gather.5.cloned.1.call-start
  7.2 1.0 broadcast_in_dim.4
  8.2 40.6 %all_to_all.46 = bf16[16,75,512]{2,1,0:T(8,128)(2,1)S(1)} all-to-all(bf16[16,75,512]{2,1,0:T(8,128)(2,1)S(1)} %broadcast_in_dim.4), channel_id=1, replica_groups=mesh['vpair_0'=4,'vpair_1'=4,'rank'=16] {'rank'}, dimensions={0} | all-to-all | bytes 2457600 | tf_op jit(solution)/shard_map/all_to_all | solution.py:13
  48.8 0.7 copy.29
  49.5 1.7 reshape.68
  51.2 0.0 all-gather.5.cloned.1.call-update
  51.2 0.0 copy-start
  51.2 1.8 broadcast_in_dim.5
  53.0 5.0 %all-to-all-start.2 = ((bf16[16,8,75,75]{3,1,2,0:T(8,128)(2,1)}), bf16[16,8,75,75]{3,1,2,0:T(8,128)(2,1)S(1)}, u32[]{:S(2)}, u32[]{:S(2)}) async-start(bf16[16,8,75,75]{3,1,2,0:T(8,128)(2,1)} %broadcast_in_dim.5), calls=%async_computation.2 | async-start | bytes 4915200 | tf_op jit(solution)/shard_map/all_to_all | solution.py:13
  58.0 1.0 copy.27
  59.0 53.9 %all-to-all-done.2 = bf16[16,8,75,75]{3,1,2,0:T(8,128)(2,1)S(1)} async-done(((bf16[16,8,75,75]{3,1,2,0:T(8,128)(2,1)}), bf16[16,8,75,75]{3,1,2,0:T(8,128)(2,1)S(1)}, u32[]{:S(2)}, u32[]{:S(2)}) %all-to-all-start.2) | async-done | bytes 1440032 | tf_op jit(solution)/shard_map/all_to_all | solution.py:13
  112.9 7.0 %all-to-all-start = ((bf16[512,16,32]{0,2,1:T(8,128)(2,1)}), bf16[512,16,32]{0,2,1:T(8,128)(2,1)S(1)}, u32[]{:S(2)}, u32[]{:S(2)}) async-start(bf16[512,16,32]{0,2,1:T(8,128)(2,1)} %bitcast), calls=%async_computation | async-start | bytes 1048576 | tf_op jit(solution)/shard_map/all_to_all | solution.py:63
  119.9 1.8 copy.38
  121.7 4.2 %reshape.75 = bf16[8,75,1200]{2,1,0:T(8,128)(2,1)S(1)} reshape(bf16[8,75,16,75]{3,2,1,0:T(8,128)(2,1)} %copy.38) | data formatting | bytes 2880000 | tf_op jit(solution)/shard_map/reshape | solution.py:19
  125.9 67.6 %all-gather.5.cloned.1.call-done = bf16[16,75,8192]{2,1,0:T(8,128)(2,1)} async-done(((bf16[1,75,8192]{2,1,0:T(8,128)(2,1)}), bf16[16,75,8192]{2,1,0:T(8,128)(2,1)}) %all-gather.5.cloned.1.call-update) | async-done | bytes 19660816 | tf_op jit(solution)/shard_map/all_gather | solution.py:53
  193.5 22.4 %reshape.69 = bf16[1200,8192]{1,0:T(8,128)(2,1)} reshape(bf16[16,75,8192]{2,1,0:T(8,128)(2,1)} %all-gather.5.cloned.1.call-done) | data formatting | bytes 39321600
  215.9 2.3 fusion.4
  218.2 1.5 copy.32
  219.7 5.3 %all-to-all-start.3 = ((bf16[8,75,512]{1,0,2:T(8,128)(2,1)}), bf16[8,75,512]{1,0,2:T(8,128)(2,1)S(1)}, u32[]{:S(2)}, u32[]{:S(2)}) async-start(bf16[8,75,512]{1,0,2:T(8,128)(2,1)} %copy.32), calls=%async_computation.3 | async-start | bytes 2097152 | tf_op jit(solution)/shard_map/all_to_all | solution.py:69
  225.0 0.2 all-gather.7.cloned.1.call-start
  225.2 0.1 convert_bitcast_fusion
  225.3 0.1 copy.41
  225.4 22.3 %reshape.74 = bf16[1200,8192,1]{1,0,2:T(8,128)(2,1)} reshape(bf16[16,75,8192]{2,1,0:T(8,128)(2,1)} %all-gather.5.cloned.1.call-done) | data formatting | bytes 39321600
  247.8 0.7 copy.34
  248.5 2.2 all_to_all.39
  250.6 17.1 %fusion.3 = bf16[8,1200,32]{1,2,0:T(8,128)(2,1)S(1)} fusion(bf16[1200,8192,1]{1,0,2:T(8,128)(2,1)} %reshape.74, bf16[8,1200,32]{1,2,0:T(8,128)(2,1)} %all_to_all.39, f32[8192,32]{0,1:T(8,128)S(1)} %bitcast.116), kind=kOutput, calls=%fused_computation.6 | convolution fusion | flops 10070831104 | bytes 21938176 | tf_op jit(solution)/shard_map/ap,ipq->iaq/dot_general | solution.py:73
  267.8 0.1 fusion.23
  267.9 0.1 fusion.22
  268.0 0.1 fusion.21
  268.1 0.1 fusion.20
  268.2 0.1 fusion.19
  268.3 0.1 fusion.18
  268.4 0.1 fusion.17
  268.5 0.1 fusion.16
  268.6 0.1 fusion.15
  268.7 0.1 fusion.14
  268.8 0.1 fusion.13
  268.9 0.1 fusion.12
  269.0 0.1 fusion.11
  269.1 0.1 fusion.10
  269.2 0.1 fusion.9
  269.3 23.4 %all_to_all.47 = bf16[16,8,75,32]{2,3,1,0:T(8,128)(2,1)S(1)} all-to-all(bf16[16,8,75,32]{2,3,1,0:T(8,128)(2,1)S(1)} %fusion.9), channel_id=1, replica_groups=mesh['vpair_0'=4,'vpair_1'=4,'rank'=16] {'vpair_0','vpair_1'}, dimensions={0} | all-to-all | bytes 1228800 | tf_op jit(solution)/shard_map/all_to_all | solution.py:77
  292.7 0.5 copy.35
  293.2 0.8 dot_general.17
  294.0 2.4 fusion.6
  296.4 0.2 pad.4
  296.6 0.0 copy-start.4
  296.6 30.2 %fusion = f32[40,1200]{1,0:T(8,128)S(1)} fusion(f32[608,1200]{1,0:T(8,128)S(1)} %pad.4), kind=kCustom, calls=%all-reduce-scatter | all-reduce-scatter fusion | flops 768001 | bytes 3111424
  326.9 1.9 collective-permute-start
  328.8 0.6 dynamic-slice.4
  330.1 3.5 collective-permute-done
  333.5 0.2 concatenate
  333.7 0.7 dynamic-slice_bitcast_fusion
  334.4 0.0 all-gather.7.cloned.1.call-update
  334.5 0.1 dynamic_slice.7
  334.6 0.9 broadcast_add_fusion
  335.4 40.0 %all-gather.7.cloned.1.call-done = f32[16,38,1200]{2,1,0:T(8,128)} async-done(((f32[1,38,1200]{2,1,0:T(8,128)}), f32[16,38,1200]{2,1,0:T(8,128)}) %all-gather.7.cloned.1.call-update) | async-done | bytes 2918416 | tf_op jit(solution)/shard_map/all_gather | solution.py:36
  375.4 2.1 reshape.71
  377.5 1.8 slice.4
  379.4 3.9 reshape.66
  383.3 4.8 %multiply_reduce_fusion = (f32[]{:T(128)}, f32[8,75,1200]{2,1,0:T(8,128)S(1)}) fusion(f32[8]{0:T(128)S(1)} %copy-done.3, f32[75,1200]{1,0:T(8,128)} %broadcast_add_fusion, f32[8,75,1200]{2,1,0:T(8,128)} %reshape.66, f32[8,75,1200]{2,0,1:T(8,128)} %param.9), kind=kLoop, calls=%fused_computation.4 | loop fusion | flops 3599999 | bytes 9000036 | tf_op jit(solution)/shard_map/reduce_sum | solution.py:94
  388.1 11.0 %psum.14 = f32[]{:T(128)} all-reduce(f32[]{:T(128)} %get-tuple-element.8), channel_id=1, replica_groups=mesh['vpair_0'=4,'vpair_1'=4,'rank'=16] {'vpair_0'}, use_global_device_ids=true, to_apply=%region_2.3 | all-reduce | flops 1 | bytes 8 | tf_op jit(solution)/shard_map/psum | solution.py:42
  399.1 3.4 copy.37
  402.5 11.1 %psum.15 = f32[]{:T(128)} all-reduce(f32[]{:T(128)} %psum.14), channel_id=1, replica_groups=mesh['vpair_0'=4,'vpair_1'=4,'rank'=16] {'vpair_1'}, use_global_device_ids=true, to_apply=%region_3.4 | all-reduce | flops 1 | bytes 8 | tf_op jit(solution)/shard_map/psum | solution.py:42
  (12 shorter events, 0.1 us)
Async XLA Ops:
  7.2 186.3 %all-gather.5.cloned.1.call-start = ((), (), s32[]{:S(2)}) async-start(), calls=%async_computation.5 | async-start | bytes 22282240 | tf_op jit(solution)/shard_map/all_gather | solution.py:53
  48.8 2.4 copy-start.1
  51.2 6.7 %copy-start = (bf16[512,512]{1,0:T(8,128)(2,1)S(1)}, bf16[512,512]{1,0:T(8,128)(2,1)}, u32[]{:S(2)}) copy-start(bf16[512,512]{1,0:T(8,128)(2,1)} %param.8) | copy-start | bytes 1572868
  53.0 59.9 %all-to-all-start.2 = ((bf16[16,8,75,75]{3,1,2,0:T(8,128)(2,1)}), bf16[16,8,75,75]{3,1,2,0:T(8,128)(2,1)S(1)}, u32[]{:S(2)}, u32[]{:S(2)}) async-start(bf16[16,8,75,75]{3,1,2,0:T(8,128)(2,1)} %broadcast_in_dim.5), calls=%async_computation.2 | async-start | bytes 4915200 | tf_op jit(solution)/shard_map/all_to_all | solution.py:13
  112.9 106.9 %all-to-all-start = ((bf16[512,16,32]{0,2,1:T(8,128)(2,1)}), bf16[512,16,32]{0,2,1:T(8,128)(2,1)S(1)}, u32[]{:S(2)}, u32[]{:S(2)}) async-start(bf16[512,16,32]{0,2,1:T(8,128)(2,1)} %bitcast), calls=%async_computation | async-start | bytes 1048576 | tf_op jit(solution)/shard_map/all_to_all | solution.py:63
  219.7 28.1 %all-to-all-start.3 = ((bf16[8,75,512]{1,0,2:T(8,128)(2,1)}), bf16[8,75,512]{1,0,2:T(8,128)(2,1)S(1)}, u32[]{:S(2)}, u32[]{:S(2)}) async-start(bf16[8,75,512]{1,0,2:T(8,128)(2,1)} %copy.32), calls=%async_computation.3 | async-start | bytes 2097152 | tf_op jit(solution)/shard_map/all_to_all | solution.py:69
  225.0 150.4 %all-gather.7.cloned.1.call-start = ((), (), s32[]{:S(2)}) async-start(), calls=%async_computation.6 | async-start | bytes 3481600 | tf_op jit(solution)/shard_map/all_gather | solution.py:36
  296.6 32.2 %copy-start.4 = (u32[256]{0:T(256)S(1)}, u32[256]{0:T(256)}, u32[]{:S(2)}) copy-start(u32[256]{0:T(256)} %constant.40) | copy-start | bytes 3076
  296.6 37.9 %copy-start.2 = (f32[1200]{0:T(1024)S(1)}, f32[1200]{0:T(1024)}, u32[]{:S(2)}) copy-start(f32[1200]{0:T(1024)} %param.10) | copy-start | bytes 14404
  326.9 6.6 %collective-permute-start = (f32[30,1200]{1,0:T(8,128)S(1)}, f32[30,1200]{1,0:T(8,128)S(1)}, u32[]{:S(2)}, u32[]{:S(2)}) collective-permute-start(f32[30,1200]{1,0:T(8,128)S(1)} %slice.5), channel_id=1, source_target_pairs={{0,1},{1,2},{2,3},{3,4},{4,5},{5,6},{6,7},{7,8},{8,9},{9,10},{10,1... | collective-permute-start | bytes 432008
  379.4 3.9 copy-start.3
Sparse Core Ops, SparseCore 0:
  51.3 142.0 all-gather.4
  334.6 40.7 all-gather.6
